TPU v7x, 32 devices: a whole 2x2x4 slice. The times are simulated.
32 devices in a mesh: row: 4 (over x, core), col: 2 (over y), depth: 4 (over z).
Axes of the slice: x: 2, y: 2, z: 4, core: 2. Of those that a mesh axis runs over, the one named last changes fastest.
Arguments:
- diag_two: float32 [256, 256], replicated, may hold values from -3 to 3, as said below
- diag_one: float32 [256, 256], replicated, may hold values from -3 to 3, as said below
- cross_tile: float32 [256, 256], replicated, may hold values from -0.375 to 0.375
- left_two: float32 [256, 4096], P(None, ('col', 'depth')), may hold values from -0.375 to 0.375
- left_one: float32 [256, 4096], P(None, ('col', 'depth')), may hold values from -0.375 to 0.375
- below_left: float32 [4096, 4096], P('row', ('col', 'depth')), may hold values from -0.09375 to 0.09375
- panel_two: float32 [4096, 256], P('row', 'col'), may hold values from -0.09375 to 0.09375
- panel_one: float32 [4096, 256], P('row', 'col'), may hold values from -0.09375 to 0.09375
- grad_diag_two: float32 [256, 256], replicated, may hold values from -6 to 6
- grad_diag_one: float32 [256, 256], replicated, may hold values from -6 to 6
- grad_cross: float32 [256, 256], replicated, may hold values from -6 to 6
- grad_left_two: float32 [256, 4096], P('row', ('col', 'depth')), may hold values from -6 to 6
- grad_left_one: float32 [256, 4096], P('row', ('col', 'depth')), may hold values from -6 to 6
- grad_below: float32 [4096, 4096], P('row', ('col', 'depth')), may hold values from -6 to 6
- grad_panel_two: float32 [4096, 256], P('row', 'col'), may hold values from -6 to 6
- grad_panel_one: float32 [4096, 256], P('row', 'col'), may hold values from -6 to 6
Outputs:
- out_below: float32 [4096, 4096], P('row', ('col', 'depth'))
- out_left_two: float32 [256, 4096], P('row', ('col', 'depth'))
- out_left_one: float32 [256, 4096], P('row', ('col', 'depth'))
- out_diag_two: float32 [256, 256], replicated
- out_diag_one: float32 [256, 256], replicated
- out_cross: float32 [256, 256], replicated
- out_panel_two: float32 [4096, 256], P('row', 'col')
- out_panel_one: float32 [4096, 256], P('row', 'col')
Inputs may be any that keep to these rules, and one draw needn't show every extreme that they name: `diag_two`: lower triangular; its diagonal lies in 1 to 3. `diag_one`: lower triangular; its diagonal lies in 1 to 3.
All inputs are finite; a program needn't handle non-finite values.
Results may differ from a plain program's by a relative error of at most 0.000071.
Values sent between devices are 32-bit elements; how exact they have to be, the bound alone decides.
A program may use at most 64 MiB of HBM per device.

v0:
```python
import jax
import jax.numpy as jnp
from jax import lax
from jax.experimental import pallas as pl
from jax.experimental.pallas import tpu as pltpu
from jax.sharding import PartitionSpec as P


def large(left, right, contract):
    return lax.dot_general(
        left,
        right,
        ((contract[:1], contract[1:]), ((), ())),
        precision=lax.Precision.HIGH,
        preferred_element_type=jnp.float32,
    )


def small(left, right, contract=(1, 0)):
    return lax.dot_general(
        left,
        right,
        ((contract[:1], contract[1:]), ((), ())),
        precision=lax.Precision.HIGHEST,
        preferred_element_type=jnp.float32,
    )


def grid_of(size):
    rows = lax.broadcasted_iota(jnp.int32, (size, size), 0)
    cols = lax.broadcasted_iota(jnp.int32, (size, size), 1)
    return rows, cols


def invert_all(blocks):
    size = blocks[0].shape[0]
    rows, cols = grid_of(size)
    apart = rows ^ cols
    lower = rows > cols
    inverses = []
    for block in blocks:
        diagonal = jnp.where(rows == cols, block, 0.0)
        down = 1.0 / jnp.sum(diagonal, axis=1, keepdims=True)
        across = 1.0 / jnp.sum(diagonal, axis=0, keepdims=True)
        pair = jnp.where(lower & (apart == 1), block, 0.0)
        inverses.append(jnp.where(rows == cols, down, 0.0) - pair * down * across)
    level = 1
    while (2 << level) <= size:
        mask = lower & ((apart >> level) == 1)
        steps = [
            small(jnp.where(mask, block, 0.0), inverse) for block, inverse in zip(blocks, inverses)
        ]
        inverses = [inverse - small(inverse, step) for inverse, step in zip(inverses, steps)]
        level += 1
    return inverses


def invert_kernel(two_ref, one_ref, cross_ref, inv_two_ref, inv_one_ref, cross_inv_ref):
    half = two_ref.shape[0] // 2
    refs = (two_ref, one_ref)
    outs = (inv_two_ref, inv_one_ref)
    blocks = []
    for ref in refs:
        blocks += [ref[:half, :half], ref[half:, half:]]
    inverses = invert_all(blocks)
    steps = [small(ref[half:, :half], inverses[2 * at]) for at, ref in enumerate(refs)]
    for at, out in enumerate(outs):
        out[:half, :half] = inverses[2 * at]
        out[half:, half:] = inverses[2 * at + 1]
        out[:half, half:] = jnp.zeros((half, half), jnp.float32)
        out[half:, :half] = -small(inverses[2 * at + 1], steps[at])
    cross_inv_ref[...] = small(cross_ref[...], inv_one_ref[...])


def chain_kernel(
    two_ref,
    one_ref,
    cross_ref,
    inv_two_ref,
    inv_one_ref,
    grad_two_ref,
    grad_one_ref,
    grad_cross_ref,
    place_ref,
    *rest,
):
    grams, outs = rest[:-5], rest[-5:]
    chain(
        two_ref,
        one_ref,
        cross_ref,
        inv_two_ref,
        inv_one_ref,
        grad_two_ref,
        grad_one_ref,
        grad_cross_ref,
        joined(grams, place_ref),
        *outs,
    )


def joined(grams, place_ref):
    if len(grams) == 1:
        return grams[0][...]
    mine, beside, twin, across = [gram[...] for gram in grams]
    left = place_ref[0] == 0
    upper = place_ref[1] == 0
    own = jnp.concatenate([jnp.where(left, mine, beside), jnp.where(left, beside, mine)], axis=1)
    far = jnp.concatenate([jnp.where(left, twin, across), jnp.where(left, across, twin)], axis=1)
    return jnp.concatenate([jnp.where(upper, own, far), jnp.where(upper, far, own)], axis=0)


def chain(
    two_ref,
    one_ref,
    cross_ref,
    inv_two_ref,
    inv_one_ref,
    grad_two_ref,
    grad_one_ref,
    grad_cross_ref,
    grams,
    sym_two_ref,
    sym_one_ref,
    half_two_ref,
    half_one_ref,
    out_cross_ref,
):
    size = two_ref.shape[0]
    rows, cols = grid_of(size)
    lower = rows >= cols
    scale = jnp.where(rows > cols, 1.0, jnp.where(rows == cols, 0.5, 0.0))

    def sym(factor, inverse, cotangent):
        inner = scale * small(factor, cotangent, (0, 0))
        spread = small(small(inverse, inner, (0, 0)), inverse)
        return spread + spread.T

    gram_two = grams[:size, :]
    gram_cross = grams[size : 2 * size, :]
    gram_below = grams[2 * size :, :]
    sym_two = sym(
        two_ref[...], inv_two_ref[...], grad_two_ref[...] - jnp.where(lower, gram_two, 0.0)
    )
    sym_two_ref[...] = sym_two
    half_two_ref[...] = scale * sym_two
    cross_next = grad_cross_ref[...] - gram_cross - small(sym_two, cross_ref[...])
    out_cross = small(cross_next, inv_one_ref[...])
    out_cross_ref[...] = out_cross
    gram_one = small(out_cross, cross_ref[...], (0, 0)) + gram_below
    sym_one = sym(
        one_ref[...], inv_one_ref[...], grad_one_ref[...] - jnp.where(lower, gram_one, 0.0)
    )
    sym_one_ref[...] = sym_one
    half_one_ref[...] = scale * sym_one


def local_call(kernel, operands, count, flops):
    size = operands[0].shape[0]
    moved = 4 * size * size * (len(operands) + count)
    return pl.pallas_call(
        kernel,
        out_shape=[jax.ShapeDtypeStruct((size, size), jnp.float32)] * count,
        in_specs=[
            pl.BlockSpec(memory_space=pltpu.SMEM if operand.ndim == 1 else pltpu.VMEM)
            for operand in operands
        ],
        out_specs=[pl.BlockSpec(memory_space=pltpu.VMEM)] * count,
        cost_estimate=pl.CostEstimate(flops=flops, bytes_accessed=moved, transcendentals=0),
    )(*operands)


def swap(values, axis, bit):
    size = lax.axis_size(axis)
    return lax.ppermute(values, axis, [(at, at ^ bit) for at in range(size)])


def gathered(values, axis):
    if lax.axis_size(axis) != 2:
        return [(lax.all_gather(values, axis, axis=1, tiled=True), 0)]
    width = values.shape[1]
    at = lax.axis_index(axis)
    return [(values, at * width), (swap(values, axis, 1), (1 - at) * width)]


def parted(values):
    high = values.astype(jnp.bfloat16)
    return high, (values - high.astype(jnp.float32)).astype(jnp.bfloat16)


def product(left, right):
    (left_high, left_low), (right_high, right_low) = parted(left), parted(right)

    def single(one, other):
        return jnp.dot(one, other, preferred_element_type=jnp.float32)

    return (single(left_low, right_high) + single(left_high, right_low)) + single(
        left_high, right_high
    )


def solve_kernel(count, starts_ref, inverse_ref, *refs):
    pieces, extra, outs = refs[:count], refs[count:-count], refs[-count:]
    total = None
    for at, piece in enumerate(pieces):
        width = piece.shape[1]
        rows = inverse_ref[pl.ds(pl.multiple_of(starts_ref[at], width), width), :]
        part = product(piece[...], rows)
        total = part if total is None else total + part
    if extra:
        total = total - product(extra[0][...], extra[1][...])
    outs[0][...] = total
    if count > 1:
        width = outs[1].shape[1]
        outs[1][...] = jnp.where(starts_ref[0] == 0, total[:, :width], total[:, width:])


def solve(pieces, inverse, *extra):
    count = len(pieces)
    rows, width = pieces[0][0].shape
    size = inverse.shape[0]
    block = rows // 4
    starts = jnp.stack([jnp.asarray(start, jnp.int32) for _, start in pieces])

    def tall(columns):
        return pl.BlockSpec((block, columns), lambda step: (step, 0))

    whole = pl.BlockSpec((size, size), lambda step: (0, 0))
    widths = [size, width][:count]
    return pl.pallas_call(
        lambda *refs: solve_kernel(count, *refs),
        grid=(4,),
        out_shape=[jax.ShapeDtypeStruct((rows, columns), jnp.float32) for columns in widths],
        in_specs=[pl.BlockSpec(memory_space=pltpu.SMEM), whole]
        + [tall(values.shape[1]) for values, _ in pieces]
        + ([tall(size), whole] if extra else []),
        out_specs=[tall(columns) for columns in widths],
        cost_estimate=pl.CostEstimate(
            flops=6 * rows * size * size, bytes_accessed=12 * rows * size, transcendentals=0
        ),
    )(starts, inverse, *[values for values, _ in pieces], *extra)


def assembled(values, axis):
    size = lax.axis_size(axis)
    if size != 2:
        return lax.all_gather(values, axis, axis=1, tiled=True)
    other = swap(values, axis, 1)
    first = lax.axis_index(axis) == 0
    return jnp.concatenate(
        [jnp.where(first, values, other), jnp.where(first, other, values)], axis=1
    )


def halve(values, axis, bit):
    mine = (lax.axis_index(axis) // bit) % 2
    keep = lax.dynamic_index_in_dim(values, mine, 0, keepdims=False)
    give = lax.dynamic_index_in_dim(values, 1 - mine, 0, keepdims=False)
    return keep + swap(give, axis, bit)


def scatter_sum(values, axis):
    size = lax.axis_size(axis)
    if size & (size - 1):
        return lax.psum_scatter(values, axis, scatter_dimension=0, tiled=False)
    bit = 1
    while bit < size:
        paired = values.reshape((-1, 2) + values.shape[1:])
        values = halve(jnp.moveaxis(paired, 1, 0), axis, bit)
        bit *= 2
    return values[0]


def row_sum(values, axis, columns):
    size = lax.axis_size(axis)
    if size & (size - 1) or size < 2:
        return [assembled(lax.psum(values, axis), columns)]
    part = halve(values.reshape((2, -1) + values.shape[1:]), axis, 1)
    bit = 2
    while bit < size:
        part = part + swap(part, axis, bit)
        bit *= 2
    if lax.axis_size(columns) == 2:
        beside = swap(part, columns, 1)
        return [part, beside, swap(part, axis, 1), swap(beside, axis, 1)]
    part = assembled(part, columns)
    other = swap(part, axis, 1)
    even = lax.axis_index(axis) % 2 == 0
    return [jnp.concatenate([jnp.where(even, part, other), jnp.where(even, other, part)], axis=0)]


def body(
    diag_two,
    diag_one,
    cross_tile,
    left_two,
    left_one,
    below_left,
    panel_two,
    panel_one,
    grad_diag_two,
    grad_diag_one,
    grad_cross,
    grad_left_two,
    grad_left_one,
    grad_below,
    grad_panel_two,
    grad_panel_one,
):
    size = diag_two.shape[0]
    share = grad_left_two.shape[0]
    width = panel_two.shape[1]
    row_start = lax.axis_index("row") * share
    col_start = lax.axis_index("col") * width
    cube = 2 * size**3

    pieces_two = gathered(grad_panel_two, "col")
    pieces_one = gathered(grad_panel_one, "col")
    inv_two, inv_one, cross_inv = local_call(
        invert_kernel, (diag_two, diag_one, cross_tile), 3, 60 * cube
    )
    solved_two, *own_two = solve(pieces_two, inv_two)
    solved_one, *own_one = solve(pieces_one, inv_one, solved_two, cross_inv)
    place = jnp.stack([lax.axis_index("col"), lax.axis_index("row") % 2]).astype(jnp.int32)
    partial = jnp.concatenate(
        [
            large(solved_two, panel_two, (0, 0)),
            large(solved_two, panel_one, (0, 0)),
            large(solved_one, panel_one, (0, 0)),
        ],
        axis=0,
    )
    grams = row_sum(partial, "row", "col")
    rows = lax.axis_size("row")
    lefts = jnp.stack(
        [
            large(solved_two, below_left, (0, 0)).reshape(rows, share, -1),
            large(solved_one, below_left, (0, 0)).reshape(rows, share, -1),
        ],
        axis=1,
    )
    summed = scatter_sum(lefts, "row")
    out_below = (
        grad_below - large(solved_two, left_two, (1, 0)) - large(solved_one, left_one, (1, 0))
    )
    sym_two, sym_one, half_two, half_one, out_cross = local_call(
        chain_kernel,
        (
            diag_two,
            diag_one,
            cross_tile,
            inv_two,
            inv_one,
            grad_diag_two,
            grad_diag_one,
            grad_cross,
            place,
            *grams,
        ),
        5,
        60 * cube,
    )
    sym_two_rows = lax.dynamic_slice_in_dim(sym_two, row_start, share, 0)
    sym_one_rows = lax.dynamic_slice_in_dim(sym_one, row_start, share, 0)
    cross_rows = lax.dynamic_slice_in_dim(out_cross, row_start, share, 0)
    cross_cols = lax.dynamic_slice_in_dim(out_cross, row_start, share, 1)
    out_left_two = (
        grad_left_two
        - summed[0]
        - large(sym_two_rows, left_two, (1, 0))
        - large(cross_rows, left_one, (1, 0))
    )
    out_left_one = (
        grad_left_one
        - summed[1]
        - large(cross_cols, left_two, (0, 0))
        - large(sym_one_rows, left_one, (1, 0))
    )
    return (
        out_below,
        out_left_two,
        out_left_one,
        half_two,
        half_one,
        out_cross,
        own_two[0] if own_two else lax.dynamic_slice_in_dim(solved_two, col_start, width, 1),
        own_one[0] if own_one else lax.dynamic_slice_in_dim(solved_one, col_start, width, 1),
    )


def solution(mesh):
    panels = P("row", "col")
    lefts = P(None, ("col", "depth"))
    blocks = P("row", ("col", "depth"))
    return jax.shard_map(
        body,
        mesh=mesh,
        in_specs=(P(), P(), P(), lefts, lefts, blocks, panels, panels)
        + (P(), P(), P(), blocks, blocks, blocks, panels, panels),
        out_specs=(blocks, blocks, blocks, P(), P(), P(), panels, panels),
        check_vma=False,
    )
```

profile of v0, /device:TPU:0, one launch (start us, length us, event | category | flops | bytes accessed | tf_op | source)
XLA Modules:
  0.0 69.3 jit_solution(7672463275063512970)
XLA Ops:
  0.6 0.0 copy-start
  0.6 3.1 %collective-permute-start = (f32[1024,128]{1,0:T(8,128)}, f32[1024,128]{1,0:T(8,128)}, u32[]{:S(2)}, u32[]{:S(2)}) collective-permute-start(f32[1024,128]{1,0:T(8,128)} %refs_2_.2), channel_id=1, source_target_pairs={{0,4},{4,0},{1,5},{5,1},{2,6},{6,2},{3,7},{7,3},{8,12},{12,8},{9,1... | collective-permute-start | bytes 1572872 | tf_op jit(solution)/shard_map/ppermute | solution.py:175
  3.7 0.1 collective-permute-start.1
  3.8 0.6 pad_add_fusion.refs_0_
  4.4 0.6 pad_add_fusion.1.place_ref
  5.0 0.0 copy-start.6
  5.0 5.6 %shard_map.215 = (f32[256,256]{1,0:T(8,128)}, f32[256,256]{1,0:T(8,128)}, f32[256,256]{1,0:T(8,128)}) custom-call(f32[256,256]{1,0:T(8,128)} %two_ref.3, f32[256,256]{1,0:T(8,128)} %one_ref.3, f32[256,256]{1,0:T(8,128)} %cross_ref.3), custom_call_target="tpu_custom_call" | custom-call | flops 2013265920 | bytes 1572864 | tf_op jit(solution)/shard_map/pallas_call | solution.py:161
  10.6 6.2 %collective-permute-done.refs_3_ = f32[1024,128]{1,0:T(8,128)} collective-permute-done((f32[1024,128]{1,0:T(8,128)}, f32[1024,128]{1,0:T(8,128)}, u32[]{:S(2)}, u32[]{:S(2)}) %collective-permute-start) | collective-permute-done | bytes 524320 | tf_op jit(solution)/shard_map/ppermute | solution.py:175
  16.8 4.3 %shard_map.216 = (f32[1024,256]{1,0:T(8,128)}, f32[1024,128]{1,0:T(8,128)}) custom-call(s32[2]{0:T(128)} %pad_add_fusion.refs_0_, f32[256,256]{1,0:T(8,128)} %get-tuple-element.20.refs_1_.inv_two_ref, f32[1024,128]{1,0:T(8,128)} %refs_2_.2, f32[1024,128]{1,0:T(8,128)} %collective-permute-done.refs_3_), custom_call_target="tpu_custom_call" | custom-call | flops 402653184 | bytes 3145728 | tf_op jit(solution)/shard_map/pallas_call | solution.py:230
  21.1 0.0 copy-done.6
  21.1 2.2 %fusion.20 = f32[256,128]{1,0:T(8,128)S(1)} fusion(f32[1024,256]{1,0:T(8,128)} %get-tuple-element.21.refs_4_, f32[1024,128]{1,0:T(8,128)S(1)} %copy-done.6), kind=kOutput, calls=%fused_computation.38 | convolution fusion | flops 201326592 | bytes 1703936 | tf_op jit(solution)/shard_map/dot_general | solution.py:10
  23.3 3.7 %collective-permute-done.1.refs_3_ = f32[1024,128]{1,0:T(8,128)S(1)} collective-permute-done((f32[1024,128]{1,0:T(8,128)}, f32[1024,128]{1,0:T(8,128)S(1)}, u32[]{:S(2)}, u32[]{:S(2)}) %collective-permute-start.1) | collective-permute-done | bytes 524320 | tf_op jit(solution)/shard_map/ppermute | solution.py:175
  27.1 0.8 %copy-done.9 = f32[1024,128]{1,0:T(8,128)} copy-done((f32[1024,128]{1,0:T(8,128)}, f32[1024,128]{1,0:T(8,128)S(1)}, u32[]{:S(2)}) %copy-start.9) | copy-done | bytes 524312
  27.9 4.8 %shard_map.217 = (f32[1024,256]{1,0:T(8,128)}, f32[1024,128]{1,0:T(8,128)}) custom-call(s32[2]{0:T(128)} %pad_add_fusion.refs_0_, f32[256,256]{1,0:T(8,128)} %get-tuple-element.22.refs_1_.inv_one_ref, f32[1024,128]{1,0:T(8,128)} %refs_2_.3, f32[1024,128]{1,0:T(8,128)} %copy-done.9, f32[1024,256]{1,0:T(8,128)} %get-tuple-element.21.refs_4_, ...), custom_call_target="tpu_custom_call" | custom-call | flops 402653184 | bytes 3145728 | tf_op jit(solution)/shard_map/pallas_call | solution.py:230
  32.7 2.3 %fusion.21 = f32[256,128]{1,0:T(8,128)S(1)} fusion(f32[1024,256]{1,0:T(8,128)} %get-tuple-element.24, f32[1024,128]{1,0:T(8,128)S(1)} %copy-done.6), kind=kOutput, calls=%fused_computation.39 | convolution fusion | flops 201326592 | bytes 1703936 | tf_op jit(solution)/shard_map/dot_general | solution.py:10
  35.0 0.0 copy-done
  35.0 0.0 copy-done.2
  35.0 0.0 copy-start.1
  35.0 0.0 copy-start.8
  35.0 1.1 %fusion.18 = f32[256,512]{1,0:T(8,128)S(1)} fusion(f32[1024,256]{1,0:T(8,128)S(1)} %copy-done.2, f32[1024,512]{1,0:T(8,128)S(1)} %copy-done), kind=kOutput, calls=%fused_computation.36 | convolution fusion | flops 805306368 | bytes 3670016 | tf_op jit(solution)/shard_map/dot_general | solution.py:10
  36.1 0.1 copy-done.1
  36.2 0.1 copy-done.8
  36.4 1.0 %fusion.19 = f32[256,128]{1,0:T(8,128)S(1)} fusion(f32[1024,256]{1,0:T(8,128)S(1)} %copy-done.1, f32[1024,128]{1,0:T(8,128)S(1)} %copy-done.8), kind=kOutput, calls=%fused_computation.37 | convolution fusion | flops 201326592 | bytes 1703936 | tf_op jit(solution)/shard_map/dot_general | solution.py:10
  37.4 0.1 collective-permute-start.4
  37.5 1.1 %fusion.17 = f32[256,512]{1,0:T(8,128)S(1)} fusion(f32[1024,256]{1,0:T(8,128)S(1)} %copy-done.1, f32[1024,512]{1,0:T(8,128)S(1)} %copy-done), kind=kOutput, calls=%fused_computation.35 | convolution fusion | flops 805306368 | bytes 3670016 | tf_op jit(solution)/shard_map/dot_general | solution.py:10
  38.6 0.0 copy-start.3
  38.6 0.1 fusion.3
  38.8 0.6 collective-permute-start.2
  39.4 0.0 collective-permute-done.4
  39.4 0.0 copy-start.4
  39.4 0.0 copy-start.7
  39.4 1.8 %collective-permute-start.5 = (f32[384,128]{1,0:T(8,128)S(1)}, f32[384,128]{1,0:T(8,128)S(1)}, u32[]{:S(2)}, u32[]{:S(2)}) collective-permute-start(f32[384,128]{1,0:T(8,128)S(1)} %bitcast_add_fusion.1), channel_id=1, source_target_pairs={{0,16},{8,24},{16,0},{24,8},{1,17},{9,25},{17,1},{25,9},{2,18},{10... | collective-permute-start | bytes 589832 | tf_op jit(solution)/shard_map/ppermute | solution.py:175
  41.2 0.0 copy-done.3
  41.2 1.0 %fusion.16 = f32[1024,512]{1,0:T(8,128)S(1)} fusion(f32[1024,256]{1,0:T(8,128)S(1)} %copy-done.1, f32[256,512]{1,0:T(8,128)S(1)} %copy-done.3), kind=kOutput, calls=%fused_computation.34 | convolution fusion | flops 805306368 | bytes 3670016 | tf_op jit(solution)/shard_map/dot_general | solution.py:10
  42.2 4.1 %collective-permute-done.5 = f32[384,128]{1,0:T(8,128)S(1)} collective-permute-done((f32[384,128]{1,0:T(8,128)S(1)}, f32[384,128]{1,0:T(8,128)S(1)}, u32[]{:S(2)}, u32[]{:S(2)}) %collective-permute-start.5) | collective-permute-done | bytes 196640 | tf_op jit(solution)/shard_map/ppermute | solution.py:175
  46.3 0.0 copy-start.10
  46.3 1.8 %collective-permute-start.6 = (f32[384,128]{1,0:T(8,128)S(1)}, f32[384,128]{1,0:T(8,128)S(1)}, u32[]{:S(2)}, u32[]{:S(2)}) collective-permute-start(f32[384,128]{1,0:T(8,128)S(1)} %add.57.rest_0_), channel_id=1, source_target_pairs={{0,4},{4,0},{1,5},{5,1},{2,6},{6,2},{3,7},{7,3},{8,12},{12,8},{9,1... | collective-permute-start | bytes 589832 | tf_op jit(solution)/shard_map/ppermute | solution.py:175
  48.1 0.0 copy-done.4
  48.1 0.0 copy-done.7
  48.1 2.5 %subtract_subtract_fusion = f32[1024,512]{1,0:T(8,128)} fusion(f32[1024,512]{1,0:T(8,128)S(1)} %copy-done.7, f32[1024,512]{1,0:T(8,128)S(1)} %fusion.16, f32[1024,256]{1,0:T(8,128)S(1)} %copy-done.2, f32[256,512]{1,0:T(8,128)S(1)} %copy-done.4), kind=kOutput, calls=%fused_computation | convolution fusion | flops 806354944 | bytes 7864320 | tf_op jit(solution)/shard_map/dot_general | solution.py:10
  50.7 0.0 copy-done.10
  50.7 0.0 collective-permute-start.7
  50.7 1.7 %collective-permute-done.6.rest_1_ = f32[384,128]{1,0:T(8,128)S(1)} collective-permute-done((f32[384,128]{1,0:T(8,128)S(1)}, f32[384,128]{1,0:T(8,128)S(1)}, u32[]{:S(2)}, u32[]{:S(2)}) %collective-permute-start.6) | collective-permute-done | bytes 196640 | tf_op jit(solution)/shard_map/ppermute | solution.py:175
  52.4 0.0 collective-permute-start.8
  52.4 0.0 collective-permute-done.2
  52.4 0.1 bitcast_add_fusion
  52.5 0.0 copy-start.5
  52.5 0.8 %copy-done.5 = f32[2,2,64,512]{3,2,1,0:T(8,128)} copy-done((f32[2,2,64,512]{3,2,1,0:T(8,128)}, f32[2,2,64,512]{3,2,1,0:T(8,128)S(1)}, u32[]{:S(2)}) %copy-start.5) | copy-done | bytes 524312
  53.3 1.8 %collective-permute-start.3 = (f32[1,2,64,512]{3,2,1,0:T(8,128)S(1)}, f32[1,2,64,512]{3,2,1,0:T(8,128)}, u32[]{:S(2)}, u32[]{:S(2)}) collective-permute-start(f32[1,2,64,512]{3,2,1,0:T(8,128)S(1)} %constant_dynamic-slice_fusion), channel_id=1, source_target_pairs={{0,16},{8,24},{16,0},{24,8},{1,17},{9,25},{17,1},{25,9},{2,18},{10... | collective-permute-start | bytes 786440 | tf_op jit(solution)/shard_map/ppermute | solution.py:175
  55.1 0.0 collective-permute-done.7.rest_2_
  55.1 0.0 copy-done.14
  55.1 0.7 copy-done.15
  55.8 0.0 collective-permute-done.8.rest_3_
  55.8 7.3 %shard_map.218 = (f32[256,256]{1,0:T(8,128)}, f32[256,256]{1,0:T(8,128)}, f32[256,256]{1,0:T(8,128)}, f32[256,256]{1,0:T(8,128)}, f32[256,256]{1,0:T(8,128)}) custom-call(f32[256,256]{1,0:T(8,128)} %two_ref.3, f32[256,256]{1,0:T(8,128)} %one_ref.3, f32[256,256]{1,0:T(8,128)} %cross_ref.3, f32[256,256]{1,0:T(8,128)} %get-tuple-element.20.refs_1_.inv_two_ref, ...), custom_call_target="tpu_custom_call" | custom-call | flops 2013265920 | bytes 4718592 | tf_op jit(solution)/shard_map/pallas_call | solution.py:161
  63.1 0.0 copy-start.13
  63.1 1.2 %fusion.7 = f32[64,512]{1,0:T(8,128)S(1)} fusion(f32[256,512]{1,0:T(8,128)S(1)} %copy-done.4, f32[256,256]{1,0:T(8,128)} %get-tuple-element.27, s32[]{:T(128)S(6)} %select_n.51), kind=kOutput, calls=%fused_computation.22 | convolution fusion | flops 50331648 | bytes 720900 | tf_op jit(solution)/shard_map/dot_general | solution.py:10
  64.3 1.1 %fusion.9 = f32[64,512]{1,0:T(8,128)S(1)} fusion(f32[256,512]{1,0:T(8,128)S(1)} %copy-done.4, f32[256,256]{1,0:T(8,128)} %get-tuple-element.17, s32[]{:T(128)S(6)} %select_n.51), kind=kOutput, calls=%fused_computation.24 | convolution fusion | flops 50331648 | bytes 720900 | tf_op jit(solution)/shard_map/dot_general | solution.py:10
  65.4 0.0 collective-permute-done.3
  65.4 1.1 %dynamic-slice_add_fusion = f32[1,2,64,512]{3,2,1,0:T(8,128)S(1)} fusion(f32[1,2,64,512]{3,2,1,0:T(8,128)} %collective-permute-done.3, f32[2,2,64,512]{3,2,1,0:T(8,128)} %copy-done.5, s32[]{:T(128)S(6)} %select_n.49), kind=kLoop, calls=%fused_computation.14 | loop fusion | flops 65536 | bytes 786436 | tf_op jit(solution)/shard_map/add | solution.py:259
  66.5 0.0 copy-done.11
  66.5 0.0 copy-done.12
  66.5 1.0 %fusion = f32[64,512]{1,0:T(8,128)} fusion(f32[64,512]{1,0:T(8,128)S(1)} %fusion.7, f32[256,512]{1,0:T(8,128)S(1)} %copy-done.3, f32[64,512]{1,0:T(8,128)S(1)} %copy-done.12, f32[1,2,64,512]{3,2,1,0:T(8,128)S(1)} %dynamic-slice_add_fusion, f32[256,256]{1,0:T(8,128)S(1)} %copy-done.11, s32[]{:T(128)S(6)} %select_n.51), kind=kOutput, calls=%fused_computation.6 | convolution fusion | flops 50429952 | bytes 1179652 | tf_op jit(solution)/shard_map/dot_general | solution.py:10
  67.5 0.0 copy-done.13
  67.5 1.8 %fusion.1 = f32[64,512]{1,0:T(8,128)} fusion(f32[64,512]{1,0:T(8,128)S(1)} %fusion.9, f32[256,512]{1,0:T(8,128)S(1)} %copy-done.3, f32[64,512]{1,0:T(8,128)S(1)} %copy-done.13, f32[1,2,64,512]{3,2,1,0:T(8,128)S(1)} %dynamic-slice_add_fusion, f32[256,256]{1,0:T(8,128)} %get-tuple-element.25, s32[]{:T(128)S(6)} %select_n.51), kind=kOutput, calls=%fused_computation.8 | convolution fusion | flops 50429952 | bytes 1114116 | tf_op jit(solution)/shard_map/dot_general | solution.py:10
  (12 shorter events, 0.2 us)
Async XLA Ops:
  0.6 34.4 %copy-start = (f32[1024,512]{1,0:T(8,128)S(1)}, f32[1024,512]{1,0:T(8,128)}, u32[]{:S(2)}) copy-start(f32[1024,512]{1,0:T(8,128)} %param.21) | copy-start | bytes 6291460
  0.6 16.2 %collective-permute-start = (f32[1024,128]{1,0:T(8,128)}, f32[1024,128]{1,0:T(8,128)}, u32[]{:S(2)}, u32[]{:S(2)}) collective-permute-start(f32[1024,128]{1,0:T(8,128)} %refs_2_.2), channel_id=1, source_target_pairs={{0,4},{4,0},{1,5},{5,1},{2,6},{6,2},{3,7},{7,3},{8,12},{12,8},{9,1... | collective-permute-start | bytes 1572872 | tf_op jit(solution)/shard_map/ppermute | solution.py:175
  3.7 23.4 %collective-permute-start.1 = (f32[1024,128]{1,0:T(8,128)}, f32[1024,128]{1,0:T(8,128)S(1)}, u32[]{:S(2)}, u32[]{:S(2)}) collective-permute-start(f32[1024,128]{1,0:T(8,128)} %refs_2_.3), channel_id=1, source_target_pairs={{0,4},{4,0},{1,5},{5,1},{2,6},{6,2},{3,7},{7,3},{8,12},{12,8},{9,1... | collective-permute-start | bytes 1572872 | tf_op jit(solution)/shard_map/ppermute | solution.py:175
  5.0 16.2 %copy-start.6 = (f32[1024,128]{1,0:T(8,128)S(1)}, f32[1024,128]{1,0:T(8,128)}, u32[]{:S(2)}) copy-start(f32[1024,128]{1,0:T(8,128)} %param.23) | copy-start | bytes 1572868
  27.1 0.8 %copy-start.9 = (f32[1024,128]{1,0:T(8,128)}, f32[1024,128]{1,0:T(8,128)S(1)}, u32[]{:S(2)}) copy-start(f32[1024,128]{1,0:T(8,128)S(1)} %collective-permute-done.1.refs_3_) | copy-start | bytes 1572868
  32.7 2.3 %copy-start.2 = (f32[1024,256]{1,0:T(8,128)S(1)}, f32[1024,256]{1,0:T(8,128)}, u32[]{:S(2)}) copy-start(f32[1024,256]{1,0:T(8,128)} %get-tuple-element.24) | copy-start | bytes 3145732
  35.0 1.2 %copy-start.1 = (f32[1024,256]{1,0:T(8,128)S(1)}, f32[1024,256]{1,0:T(8,128)}, u32[]{:S(2)}) copy-start(f32[1024,256]{1,0:T(8,128)} %get-tuple-element.21.refs_4_) | copy-start | bytes 3145732
  35.0 1.3 %copy-start.8 = (f32[1024,128]{1,0:T(8,128)S(1)}, f32[1024,128]{1,0:T(8,128)}, u32[]{:S(2)}) copy-start(f32[1024,128]{1,0:T(8,128)} %param.22) | copy-start | bytes 1572868
  37.4 1.9 %collective-permute-start.4 = (f32[384,128]{1,0:T(8,128)S(1)}, f32[384,128]{1,0:T(8,128)S(1)}, u32[]{:S(2)}, u32[]{:S(2)}) collective-permute-start(f32[384,128]{1,0:T(8,128)S(1)} %dynamic-slice_bitcast_fusion), channel_id=1, source_target_pairs={{0,8},{8,0},{16,24},{24,16},{1,9},{9,1},{17,25},{25,17},{2,10},{10... | collective-permute-start | bytes 589832 | tf_op jit(solution)/shard_map/ppermute | solution.py:175
  38.6 2.6 %copy-start.3 = (f32[256,512]{1,0:T(8,128)S(1)}, f32[256,512]{1,0:T(8,128)}, u32[]{:S(2)}) copy-start(f32[256,512]{1,0:T(8,128)} %param.19) | copy-start | bytes 1572868
  38.8 13.6 %collective-permute-start.2 = (f32[2,2,64,512]{3,2,1,0:T(8,128)S(1)}, f32[2,2,64,512]{3,2,1,0:T(8,128)S(1)}, u32[]{:S(2)}, u32[]{:S(2)}) collective-permute-start(f32[2,2,64,512]{3,2,1,0:T(8,128)S(1)} %bitcast.50), channel_id=1, source_target_pairs={{0,8},{8,0},{16,24},{24,16},{1,9},{9,1},{17,25},{25,17},{2,10},{10... | collective-permute-start | bytes 1572872 | tf_op jit(solution)/shard_map/ppermute | solution.py:175
  39.4 8.8 %copy-start.4 = (f32[256,512]{1,0:T(8,128)S(1)}, f32[256,512]{1,0:T(8,128)}, u32[]{:S(2)}) copy-start(f32[256,512]{1,0:T(8,128)} %param.20) | copy-start | bytes 1572868
  39.4 8.8 %copy-start.7 = (f32[1024,512]{1,0:T(8,128)S(1)}, f32[1024,512]{1,0:T(8,128)}, u32[]{:S(2)}) copy-start(f32[1024,512]{1,0:T(8,128)} %param.29) | copy-start | bytes 6291460
  39.4 6.9 %collective-permute-start.5 = (f32[384,128]{1,0:T(8,128)S(1)}, f32[384,128]{1,0:T(8,128)S(1)}, u32[]{:S(2)}, u32[]{:S(2)}) collective-permute-start(f32[384,128]{1,0:T(8,128)S(1)} %bitcast_add_fusion.1), channel_id=1, source_target_pairs={{0,16},{8,24},{16,0},{24,8},{1,17},{9,25},{17,1},{25,9},{2,18},{10... | collective-permute-start | bytes 589832 | tf_op jit(solution)/shard_map/ppermute | solution.py:175
  46.3 4.4 %copy-start.10 = (f32[384,128]{1,0:T(8,128)}, f32[384,128]{1,0:T(8,128)S(1)}, u32[]{:S(2)}) copy-start(f32[384,128]{1,0:T(8,128)S(1)} %add.57.rest_0_) | copy-start | bytes 589828
  46.3 6.0 %collective-permute-start.6 = (f32[384,128]{1,0:T(8,128)S(1)}, f32[384,128]{1,0:T(8,128)S(1)}, u32[]{:S(2)}, u32[]{:S(2)}) collective-permute-start(f32[384,128]{1,0:T(8,128)S(1)} %add.57.rest_0_), channel_id=1, source_target_pairs={{0,4},{4,0},{1,5},{5,1},{2,6},{6,2},{3,7},{7,3},{8,12},{12,8},{9,1... | collective-permute-start | bytes 589832 | tf_op jit(solution)/shard_map/ppermute | solution.py:175
  50.7 4.4 %collective-permute-start.7 = (f32[384,128]{1,0:T(8,128)S(1)}, f32[384,128]{1,0:T(8,128)S(1)}, u32[]{:S(2)}, u32[]{:S(2)}) collective-permute-start(f32[384,128]{1,0:T(8,128)S(1)} %add.57.rest_0_), channel_id=1, source_target_pairs={{0,8},{8,0},{16,24},{24,16},{1,9},{9,1},{17,25},{25,17},{2,10},{10... | collective-permute-start | bytes 589832 | tf_op jit(solution)/shard_map/ppermute | solution.py:175
  52.4 2.7 %copy-start.14 = (f32[384,128]{1,0:T(8,128)}, f32[384,128]{1,0:T(8,128)S(1)}, u32[]{:S(2)}) copy-start(f32[384,128]{1,0:T(8,128)S(1)} %collective-permute-done.6.rest_1_) | copy-start | bytes 589828
  52.4 3.4 %collective-permute-start.8 = (f32[384,128]{1,0:T(8,128)S(1)}, f32[384,128]{1,0:T(8,128)}, u32[]{:S(2)}, u32[]{:S(2)}) collective-permute-start(f32[384,128]{1,0:T(8,128)S(1)} %collective-permute-done.6.rest_1_), channel_id=1, source_target_pairs={{0,8},{8,0},{16,24},{24,16},{1,9},{9,1},{17,25},{25,17},{2,10},{10... | collective-permute-start | bytes 589832 | tf_op jit(solution)/shard_map/ppermute | solution.py:175
  52.5 0.8 %copy-start.5 = (f32[2,2,64,512]{3,2,1,0:T(8,128)}, f32[2,2,64,512]{3,2,1,0:T(8,128)S(1)}, u32[]{:S(2)}) copy-start(f32[2,2,64,512]{3,2,1,0:T(8,128)S(1)} %bitcast_add_fusion) | copy-start | bytes 1572868
  53.3 12.1 %collective-permute-start.3 = (f32[1,2,64,512]{3,2,1,0:T(8,128)S(1)}, f32[1,2,64,512]{3,2,1,0:T(8,128)}, u32[]{:S(2)}, u32[]{:S(2)}) collective-permute-start(f32[1,2,64,512]{3,2,1,0:T(8,128)S(1)} %constant_dynamic-slice_fusion), channel_id=1, source_target_pairs={{0,16},{8,24},{16,0},{24,8},{1,17},{9,25},{17,1},{25,9},{2,18},{10... | collective-permute-start | bytes 786440 | tf_op jit(solution)/shard_map/ppermute | solution.py:175
  55.1 0.7 copy-start.15
  63.1 3.4 %copy-start.11 = (f32[256,256]{1,0:T(8,128)S(1)}, f32[256,256]{1,0:T(8,128)}, u32[]{:S(2)}) copy-start(f32[256,256]{1,0:T(8,128)} %get-tuple-element.17) | copy-start | bytes 786436
  63.1 3.4 %copy-start.12 = (f32[64,512]{1,0:T(8,128)S(1)}, f32[64,512]{1,0:T(8,128)}, u32[]{:S(2)}) copy-start(f32[64,512]{1,0:T(8,128)} %param.28) | copy-start | bytes 393220
  63.1 4.4 %copy-start.13 = (f32[64,512]{1,0:T(8,128)S(1)}, f32[64,512]{1,0:T(8,128)}, u32[]{:S(2)}) copy-start(f32[64,512]{1,0:T(8,128)} %param.27) | copy-start | bytes 393220
where the time goes:
time: 69.8 us; the launch traced here: 69.3 us
  Pallas kernels  22 us (32%)
  matrix products  16.3 us (23%)
  waiting for transfers between devices  15.8 us (23%)
  starting transfers between devices  9.13 us (13%)
  local copies, waits for them, and re-layouts  2.66 us (4%)
  other arithmetic  2.49 us (4%)
  between operations  0.88 us (1%)
    dot_general x11, matrix products, large(): lax.dot_general(left, right, ((contract[:1], contract[1:]), ((), ())), pr...  16.3 us
    ppermute x9, waiting for transfers between devices, swap(): return lax.ppermute(values, axis, [(at, at ^ bit) for at in range(size)])  15.8 us
    pallas_call x2, Pallas kernels, local_call(): pl.pallas_call(kernel, out_shape=[jax.ShapeDtypeStruct((size, size), jnp....  12.9 us
    ppermute x9, starting transfers between devices, swap(): return lax.ppermute(values, axis, [(at, at ^ bit) for at in range(size)])  9.13 us
    pallas_call x2, Pallas kernels, solve(): pl.pallas_call(lambda *refs: solve_kernel(count, *refs), grid=(4,), out_s...  9.12 us
    unnamed x32, local copies, waits for them, and re-layouts  2.59 us
  transfers between devices with their start and end apart: 9, of which 4 were waited for; matrix products, arithmetic and copies ran while one was open for 15% of the time, Pallas kernels for 25%

commit v1 on v0

--- a/solution.py
+++ b/solution.py
@@ -388,12 +388,605 @@
     )
 
 
+MESH = pl.DeviceIdType.MESH
+
+
+def split(values):
+    high = values.astype(jnp.bfloat16)
+    return high, (values - high.astype(jnp.float32)).astype(jnp.bfloat16)
+
+
+def thrice(left, right, contract=(1, 0)):
+    def single(one, other):
+        return lax.dot_general(
+            one,
+            other,
+            ((contract[:1], contract[1:]), ((), ())),
+            preferred_element_type=jnp.float32,
+        )
+
+    return (single(left[1], right[0]) + single(left[0], right[1])) + single(left[0], right[0])
+
+
+def fused_kernel(chunks, *refs):
+    (
+        two_hbm,
+        one_hbm,
+        cross_hbm,
+        left_two_hbm,
+        left_one_hbm,
+        below_hbm,
+        panel_two_hbm,
+        panel_one_hbm,
+        grad_two_hbm,
+        grad_one_hbm,
+        grad_cross_hbm,
+        grad_left_two_hbm,
+        grad_left_one_hbm,
+        grad_below_hbm,
+        grad_panel_two_hbm,
+        grad_panel_one_hbm,
+    ) = refs[:16]
+    (
+        out_below,
+        out_left_two,
+        out_left_one,
+        out_diag_two,
+        out_diag_one,
+        out_cross,
+        out_panel_two,
+        out_panel_one,
+    ) = refs[16:24]
+    (
+        two,
+        one,
+        cross,
+        left,
+        below,
+        panels,
+        grad_two,
+        grad_one,
+        grad_cross,
+        grad_left,
+        acc,
+        full_two,
+        full_one,
+        solved,
+        solved_high,
+        solved_low,
+        left_high,
+        left_low,
+        below_high,
+        below_low,
+        inverses,
+        crossed,
+        pre,
+        partial,
+        from_core,
+        chip,
+        from_x,
+        own,
+        oth,
+        lefts,
+        lefts_core,
+        lefts_send,
+        lefts_x,
+        sym,
+        next_cross,
+        cross_t,
+        halves,
+        panel_out,
+        load_sem,
+        store_sem,
+        y_send,
+        y_recv,
+        z_send,
+        z_recv,
+        w_send,
+        w_recv,
+        l_send,
+        l_recv,
+    ) = refs[24:]
+    size = two.shape[0]
+    rows, width = grad_panel_two_hbm.shape
+    share = grad_left.shape[1]
+    half = rows // 2
+    step = half // chunks
+    quarter = width // 2
+    at_row, at_col, at_depth = (lax.axis_index(name) for name in ("row", "col", "depth"))
+    core = lax.rem(at_row, 2)
+    side = lax.div(at_row, 2)
+    first = at_col == 0
+    part = lax.rem(at_depth, 2)
+    to_core = (at_row + 1 - 2 * core, at_col, at_depth)
+    to_x = (at_row + 2 - 4 * side, at_col, at_depth)
+    to_y = (at_row, 1 - at_col, at_depth)
+    to_z = (at_row, at_col, at_depth + 1 - 2 * part)
+
+    loads = []
+
+    def load(source, target):
+        copy = pltpu.make_async_copy(source, target, load_sem.at[len(loads)])
+        copy.start()
+        loads.append(copy)
+        return copy
+
+    own_two = load(grad_panel_two_hbm, full_two.at[:, :width])
+    pan_two = load(panel_two_hbm, panels.at[:, :width])
+    pan_one = load(panel_one_hbm, panels.at[:, width:])
+    own_one = load(grad_panel_one_hbm, full_one.at[:, :width])
+    small_loads = [
+        load(two_hbm, two),
+        load(one_hbm, one),
+        load(cross_hbm, cross),
+        load(grad_two_hbm, grad_two),
+        load(grad_one_hbm, grad_one),
+        load(grad_cross_hbm, grad_cross),
+    ]
+    below_load = load(below_hbm, below)
+    left_loads = [load(left_two_hbm, left.at[:size]), load(left_one_hbm, left.at[size:])]
+    acc_load = load(grad_below_hbm, acc)
+    grad_left_loads = [
+        load(grad_left_two_hbm, grad_left.at[0]),
+        load(grad_left_one_hbm, grad_left.at[1]),
+    ]
+
+    barrier = pltpu.get_barrier_semaphore()
+    for target in (to_core, to_x, to_y, to_z):
+        pl.semaphore_signal(barrier, inc=1, device_id=target, device_id_type=MESH)
+    pl.semaphore_wait(barrier, 4)
+
+    sends = []
+
+    def send(source, target, sems, at, device):
+        copy = pltpu.make_async_remote_copy(
+            src_ref=source,
+            dst_ref=target,
+            send_sem=sems[0].at[at],
+            recv_sem=sems[1].at[at],
+            device_id=device,
+            device_id_type=MESH,
+        )
+        copy.start()
+        sends.append(copy)
+        return copy
+
+    fulls = (full_two, full_one)
+    y_copies = []
+    for panel, source in enumerate((grad_panel_two_hbm, grad_panel_one_hbm)):
+        for at in range(chunks):
+            place = pl.ds(pl.multiple_of(part * half + at * step, step), step)
+            y_copies.append(
+                send(
+                    source.at[place, :],
+                    fulls[panel].at[place, width:],
+                    (y_send, y_recv),
+                    panel * chunks + at,
+                    to_y,
+                )
+            )
+    z_copies = []
+
+    def forward():
+        at = len(z_copies)
+        y_copies[at].wait_recv()
+        panel, chunk = divmod(at, chunks)
+        place = pl.ds(pl.multiple_of(part * half + chunk * step, step), step)
+        piece = fulls[panel].at[place, width:]
+        z_copies.append(send(piece, piece, (z_send, z_recv), at, to_z))
+
+    mine = pl.ds(pl.multiple_of(core * quarter, quarter), quarter)
+    theirs = pl.ds(pl.multiple_of((1 - core) * quarter, quarter), quarter)
+    stages = ((0, 3), (3, 2), (5, 1))
+    waits = {}
+
+    def w_core(stage):
+        start, count = stages[stage]
+        blocks = pl.ds(start, count)
+        waits["core", stage] = send(
+            partial.at[blocks, theirs, :],
+            from_core.at[blocks],
+            (w_send, w_recv),
+            stage * 5,
+            to_core,
+        )
+
+    def w_x(stage):
+        start, count = stages[stage]
+        blocks = pl.ds(start, count)
+        waits["core", stage].wait_recv()
+        chip[blocks] = partial[blocks, mine, :] + from_core[blocks]
+        waits["x", stage] = send(
+            chip.at[blocks], from_x.at[blocks], (w_send, w_recv), stage * 5 + 1, to_x
+        )
+
+    def w_y(stage):
+        start, count = stages[stage]
+        blocks = pl.ds(start, count)
+        waits["x", stage].wait_recv()
+        own[blocks, mine, :] = chip[blocks] + from_x[blocks]
+        piece = own.at[blocks, mine, :]
+        waits["y", stage] = send(
+            piece, oth.at[blocks, mine, :], (w_send, w_recv), stage * 5 + 2, to_y
+        )
+        waits["own", stage] = send(piece, piece, (w_send, w_recv), stage * 5 + 3, to_core)
+
+    def w_last(stage):
+        start, count = stages[stage]
+        blocks = pl.ds(start, count)
+        waits["y", stage].wait_recv()
+        piece = oth.at[blocks, mine, :]
+        waits["oth", stage] = send(piece, piece, (w_send, w_recv), stage * 5 + 4, to_core)
+
+    def w_done(stage):
+        waits["own", stage].wait_recv()
+        waits["oth", stage].wait_recv()
+
+    def joined_at(diagonal, off):
+        near, far = own[diagonal], oth[diagonal]
+        near_off, far_off = own[off], oth[off]
+        top = [jnp.where(first, near, far), jnp.where(first, far_off, near_off)]
+        bottom = [jnp.where(first, near_off, far_off), jnp.where(first, far, near)]
+        return jnp.concatenate(
+            [jnp.concatenate(top, axis=1), jnp.concatenate(bottom, axis=1)], axis=0
+        )
+
+    own_two.wait()
+    pan_two.wait()
+    pan_one.wait()
+    panel_parts = split(panels[...])
+    found = thrice(split(full_two[:, :width]), panel_parts, (0, 0))
+    partial[0] = found[:, :width]
+    partial[1] = found[:, width:]
+    own_one.wait()
+    partial[2] = thrice(
+        split(full_one[:, :width]), tuple(piece[:, width:] for piece in panel_parts), (0, 0)
+    )
+    w_core(0)
+
+    for copy in small_loads:
+        copy.wait()
+    grid_rows, grid_cols = grid_of(size)
+    scale = jnp.where(
+        grid_rows > grid_cols, 1.0, jnp.where(grid_rows == grid_cols, 0.5, 0.0)
+    )
+    events = {1: forward, 2: lambda: w_x(0), 3: forward, 5: forward, 6: lambda: w_y(0)}
+    mid = size // 2
+    blocks = []
+    for ref in (two, one):
+        blocks += [ref[:mid, :mid], ref[mid:, mid:]]
+    found = invert_steps(blocks, events)
+    for at, ref in enumerate((two, one)):
+        step_product = small(ref[mid:, :mid], found[2 * at])
+        inverses[at, :mid, :mid] = found[2 * at]
+        inverses[at, mid:, mid:] = found[2 * at + 1]
+        inverses[at, :mid, mid:] = jnp.zeros((mid, size - mid), jnp.float32)
+        inverses[at, mid:, :mid] = -small(found[2 * at + 1], step_product)
+    while len(z_copies) < chunks:
+        forward()
+
+    def local_rows(values):
+        near = jnp.where(first, values[:width, :], values[width:, :])
+        away = jnp.where(first, values[width:, :], values[:width, :])
+        return jnp.concatenate([near, away], axis=0)
+
+    inverse_two = inverses[0]
+    right_two = split(local_rows(inverse_two))
+
+    def solve_two(begin):
+        place = pl.ds(pl.multiple_of(begin, half), half)
+        pieces = split(full_two[place, :])
+        off = thrice(
+            tuple(piece[:, width:] for piece in pieces), split(panels[place, :]), (0, 0)
+        )
+        total = thrice(pieces, right_two)
+        solved[place, :size] = total
+        high, low = split(total)
+        solved_high[place, :size] = high
+        solved_low[place, :size] = low
+        return off
+
+    off_near = solve_two(part * half)
+    forward()
+    crossed[0] = small(cross[...], inverses[1])
+    crossed[1] = small(inverse_two, cross[...])
+    pre[0] = small(two[...], grad_two[...], (0, 0))
+    pre[1] = small(one[...], grad_one[...], (0, 0))
+    for at in range(chunks):
+        z_copies[at].wait_recv()
+    off_far = solve_two((1 - part) * half)
+    off = off_near + off_far
+    partial[3] = off[:, :width]
+    partial[4] = off[:, width:]
+    w_core(1)
+    forward()
+
+    stores = []
+
+    def store(source, target):
+        copy = pltpu.make_async_copy(source, target, store_sem.at[len(stores)])
+        copy.start()
+        stores.append(copy)
+
+    def own_columns(values):
+        return jnp.where(first, values[:, :width], values[:, width:])
+
+    panel_out[0] = own_columns(solved[:, :size])
+    store(panel_out.at[0], out_panel_two)
+    below_load.wait()
+    high, low = split(below[...])
+    below_high[...] = high
+    below_low[...] = low
+    for copy in left_loads:
+        copy.wait()
+    high, low = split(left[...])
+    left_high[...] = high
+    left_low[...] = low
+    w_x(1)
+    l_waits = {}
+
+    def lefts_of(panel):
+        columns = pl.ds(panel * size, size)
+        product_of = thrice(
+            (solved_high[:, columns], solved_low[:, columns]),
+            (below_high[...], below_low[...]),
+            (0, 0),
+        )
+        lefts[panel] = product_of.reshape(lefts.shape[1:])
+        for at in range(2):
+            l_waits["core", panel, at] = send(
+                lefts.at[panel, at, 1 - core],
+                lefts_core.at[panel, at],
+                (l_send, l_recv),
+                panel * 3 + at,
+                to_core,
+            )
+
+    def lefts_away(panel):
+        for at in range(2):
+            l_waits["core", panel, at].wait_recv()
+        lefts_send[panel] = lefts[panel, 1 - side, core] + lefts_core[panel, 1 - side]
+        l_waits["x", panel] = send(
+            lefts_send.at[panel], lefts_x.at[panel], (l_send, l_recv), panel * 3 + 2, to_x
+        )
+
+    def lefts_end(panel):
+        l_waits["x", panel].wait_recv()
+        return (lefts[panel, side, core] + lefts_core[panel, side]) + lefts_x[panel]
+
+    tile = rows // 4
+
+    def below_of(panel):
+        columns = pl.ds(panel * size, size)
+        rights = (left_high[columns, :], left_low[columns, :])
+        for at in range(4):
+            place = pl.ds(at * tile, tile)
+            acc[place, :] = acc[place, :] - thrice(
+                (solved_high[place, columns], solved_low[place, columns]), rights
+            )
+
+    lefts_of(0)
+    forward()
+    acc_load.wait()
+    below_of(0)
+    lefts_away(0)
+    forward()
+    w_y(1)
+
+    right_one = split(
+        jnp.concatenate([local_rows(inverses[1]), -crossed[0]], axis=0)
+    )
+
+    def solve_one(begin):
+        place = pl.ds(pl.multiple_of(begin, half), half)
+        pieces = split(full_one[place, :])
+        off = thrice(
+            tuple(piece[:, width:] for piece in pieces), split(panels[place, width:]), (0, 0)
+        )
+        lefts_of_it = tuple(
+            jnp.concatenate([piece, before[place, :size]], axis=1)
+            for piece, before in zip(pieces, (solved_high, solved_low))
+        )
+        total = thrice(lefts_of_it, right_one)
+        solved[place, size:] = total
+        high, low = split(total)
+        solved_high[place, size:] = high
+        solved_low[place, size:] = low
+        return off
+
+    off_near = solve_one(part * half)
+    w_last(0)
+    for at in range(chunks, 2 * chunks):
+        z_copies[at].wait_recv()
+    off_far = solve_one((1 - part) * half)
+    partial[5] = off_near + off_far
+    w_core(2)
+    panel_out[1] = own_columns(solved[:, size:])
+    store(panel_out.at[1], out_panel_one)
+    w_last(1)
+    w_x(2)
+    lefts_of(1)
+    w_y(2)
+    w_done(0)
+    w_done(1)
+
+    inner = scale * (pre[0] - joined_at(0, 3))
+    middle = inner + inner.T
+    cross_gram = small(inverse_two, joined_at(1, 4), (0, 0))
+    spread = small(
+        inverse_two,
+        small(middle, jnp.concatenate([inverse_two, crossed[1]], axis=1)),
+        (0, 0),
+    )
+    sym[0] = spread[:, :size]
+    halves[0] = scale * sym[0]
+    store(halves.at[0], out_diag_two)
+    following = grad_cross[...] - cross_gram - spread[:, size:]
+    next_cross[...] = small(following, inverses[1])
+    store(next_cross, out_cross)
+    cross_t[...] = next_cross[...].T
+    lefts_away(1)
+    ready = pre[1] - (
+        small(following, cross[...], (0, 0)) - small(cross[...], cross_gram, (0, 0))
+    )
+    w_last(2)
+    below_of(1)
+    store(acc, out_below)
+    mine_rows = pl.ds(pl.multiple_of(at_row * share, share), share)
+    for copy in grad_left_loads:
+        copy.wait()
+    head = split(jnp.concatenate([sym[0, mine_rows, :], next_cross[mine_rows, :]], axis=1))
+    grad_left[0] = (grad_left[0] - lefts_end(0)) - thrice(
+        head, (left_high[...], left_low[...])
+    )
+    store(grad_left.at[0], out_left_two)
+    grad_left[1] = (grad_left[1] - lefts_end(1)) - thrice(
+        split(cross_t[mine_rows, :]), (left_high[:size], left_low[:size])
+    )
+    w_done(2)
+    inner = scale * (ready - joined_at(2, 5))
+    sym[1] = small(inverses[1], small(inner + inner.T, inverses[1]), (0, 0))
+    grad_left[1] = grad_left[1] - thrice(
+        split(sym[1, mine_rows, :]), (left_high[size:], left_low[size:])
+    )
+    store(grad_left.at[1], out_left_one)
+    halves[1] = scale * sym[1]
+    store(halves.at[1], out_diag_one)
+    for copy in sends:
+        copy.wait_send()
+    for copy in stores:
+        copy.wait()
+
+
+def invert_steps(blocks, events):
+    size = blocks[0].shape[0]
+    rows, cols = grid_of(size)
+    apart = rows ^ cols
+    lower = rows > cols
+    inverses = []
+    for block in blocks:
+        diagonal = jnp.where(rows == cols, block, 0.0)
+        down = 1.0 / jnp.sum(diagonal, axis=1, keepdims=True)
+        across = 1.0 / jnp.sum(diagonal, axis=0, keepdims=True)
+        pair = jnp.where(lower & (apart == 1), block, 0.0)
+        inverses.append(jnp.where(rows == cols, down, 0.0) - pair * down * across)
+    level = 1
+    while (2 << level) <= size:
+        mask = lower & ((apart >> level) == 1)
+        steps = [
+            small(jnp.where(mask, block, 0.0), inverse) for block, inverse in zip(blocks, inverses)
+        ]
+        inverses = [inverse - small(inverse, step) for inverse, step in zip(inverses, steps)]
+        if level in events:
+            events[level]()
+        level += 1
+    for late in sorted(events):
+        if late >= level:
+            events[late]()
+    return inverses
+
+
+def fused(*arrays):
+    two, left, below, grad_left = arrays[0], arrays[3], arrays[5], arrays[11]
+    size = two.shape[0]
+    rows, width = arrays[14].shape
+    columns = below.shape[1]
+    share = grad_left.shape[0]
+    chunks = 4
+    quarter = width // 2
+
+    def real(*shape):
+        return pltpu.VMEM(shape, jnp.float32)
+
+    def short(*shape):
+        return pltpu.VMEM(shape, jnp.bfloat16)
+
+    def outs(*shape):
+        return jax.ShapeDtypeStruct(shape, jnp.float32)
+
+    scratch = [
+        real(size, size),
+        real(size, size),
+        real(size, size),
+        real(2 * size, columns),
+        real(rows, columns),
+        real(rows, size),
+        real(size, size),
+        real(size, size),
+        real(size, size),
+        real(2, share, columns),
+        real(rows, columns),
+        real(rows, size),
+        real(rows, size),
+        real(rows, 2 * size),
+        short(rows, 2 * size),
+        short(rows, 2 * size),
+        short(2 * size, columns),
+        short(2 * size, columns),
+        short(rows, columns),
+        short(rows, columns),
+        real(2, size, size),
+        real(2, size, size),
+        real(2, size, size),
+        real(6, width, width),
+        real(6, quarter, width),
+        real(6, quarter, width),
+        real(6, quarter, width),
+        real(6, width, width),
+        real(6, width, width),
+        real(2, 2, 2, share, columns),
+        real(2, 2, share, columns),
+        real(2, share, columns),
+        real(2, share, columns),
+        real(2, size, size),
+        real(size, size),
+        real(size, size),
+        real(2, size, size),
+        real(2, rows, width),
+        pltpu.SemaphoreType.DMA((16,)),
+        pltpu.SemaphoreType.DMA((8,)),
+        pltpu.SemaphoreType.DMA((2 * chunks,)),
+        pltpu.SemaphoreType.DMA((2 * chunks,)),
+        pltpu.SemaphoreType.DMA((2 * chunks,)),
+        pltpu.SemaphoreType.DMA((2 * chunks,)),
+        pltpu.SemaphoreType.DMA((15,)),
+        pltpu.SemaphoreType.DMA((15,)),
+        pltpu.SemaphoreType.DMA((6,)),
+        pltpu.SemaphoreType.DMA((6,)),
+    ]
+    anywhere = pl.BlockSpec(memory_space=pl.ANY)
+    return pl.pallas_call(
+        lambda *refs: fused_kernel(chunks, *refs),
+        out_shape=[
+            outs(rows, columns),
+            outs(share, columns),
+            outs(share, columns),
+            outs(size, size),
+            outs(size, size),
+            outs(size, size),
+            outs(rows, width),
+            outs(rows, width),
+        ],
+        in_specs=[anywhere] * 16,
+        out_specs=[anywhere] * 8,
+        scratch_shapes=scratch,
+        compiler_params=pltpu.CompilerParams(collective_id=0, has_side_effects=True),
+        cost_estimate=pl.CostEstimate(
+            flops=24 * rows * size * columns, bytes_accessed=16 * rows * columns, transcendentals=0
+        ),
+    )(*arrays)
+
+
+def fits(mesh):
+    return mesh.shape["row"] == 4 and mesh.shape["col"] == 2 and mesh.shape["depth"] % 2 == 0
+
+
 def solution(mesh):
     panels = P("row", "col")
     lefts = P(None, ("col", "depth"))
     blocks = P("row", ("col", "depth"))
     return jax.shard_map(
-        body,
+        fused if fits(mesh) else body,
         mesh=mesh,
         in_specs=(P(), P(), P(), lefts, lefts, blocks, panels, panels)
         + (P(), P(), P(), blocks, blocks, blocks, panels, panels),

time: 69.8 us -> 50.2 us (0.72)
  Pallas kernels: 22 us -> 41.1 us
  matrix products: 16.3 us -> 0 us
  waiting for transfers between devices: 15.8 us -> 0 us
  starting transfers between devices: 9.13 us -> 0 us
  local copies, waits for them, and re-layouts: 2.66 us -> 8.2 us
  other arithmetic: 2.49 us -> 0 us
    pallas_call x4 -> x1, Pallas kernels: 22 us -> 41.1 us  [fused(): pl.pallas_call(lambda *refs: fused_kernel(chunks, *refs), out_shape=[outs...]
    dot_general x11 -> x0, matrix products: 16.3 us -> none  [large(): lax.dot_general(left, right, ((contract[:1], contract[1:]), ((), ())), pr...]
    ppermute x9 -> x0, waiting for transfers between devices: 15.8 us -> none  [swap(): return lax.ppermute(values, axis, [(at, at ^ bit) for at in range(size)])]
    ppermute x9 -> x0, starting transfers between devices: 9.13 us -> none  [swap(): return lax.ppermute(values, axis, [(at, at ^ bit) for at in range(size)])]
    unnamed x32 -> x22, local copies, waits for them, and re-layouts: 2.59 us -> 8.2 us
    another operation x3 -> x0, other arithmetic: 1.27 us -> none  [the longest x1 0.58 us: solve(): starts = jnp.stack([jnp.asarray(start, jnp.int32) for _, start in pieces])]
    add x4 -> x0, other arithmetic: 1.2 us -> none  [the longest x3 1.18 us: halve(): return keep + swap(give, axis, bit)]
  transfers between devices with their start and end apart: 9 -> 0, of which waited for: 4 -> 0; matrix products, arithmetic and copies ran while one was open for 15% -> 0% of each run, Pallas kernels for 25% -> 0%
where the time goes in v1:
time: 50.2 us; the launch traced here: 50 us
  Pallas kernels  41.1 us (82%)
  local copies, waits for them, and re-layouts  8.2 us (16%)
  between operations  0.7 us (1%)
    pallas_call x1, Pallas kernels, fused(): pl.pallas_call(lambda *refs: fused_kernel(chunks, *refs), out_shape=[outs...  41.1 us
    unnamed x22, local copies, waits for them, and re-layouts  8.2 us

profile of v1, /device:TPU:0, one launch (start us, length us, event | category | flops | bytes accessed | tf_op | source)
XLA Modules:
  0.0 50.0 jit_solution(18039274004055526225)
XLA Ops:
  0.6 41.1 %shard_map.215 = (f32[1024,512]{1,0:T(8,128)}, f32[64,512]{1,0:T(8,128)}, f32[64,512]{1,0:T(8,128)}, f32[256,256]{1,0:T(8,128)}, f32[256,256]{1,0:T(8,128)}, /*i...) custom-call(f32[256,256]{1,0:T(8,128)} %refs_0_.1, f32[256,256]{1,0:T(8,128)} %refs_1_.1, ...), custom_call_target="tpu_custom_call" | custom-call | flops 3221225472 | bytes 8388608 | tf_op jit(solution)/shard_map/pallas_call | solution.py:958
  41.8 0.0 copy-start.6
  41.8 0.0 copy-start.5
  41.8 0.0 copy-start.4
  41.8 0.0 copy-start.3
  41.8 0.0 copy-start.2
  41.8 3.2 %copy.32 = f32[1024,512]{1,0:T(8,128)} copy(f32[1024,512]{1,0:T(8,128)} %get-tuple-element.16) | data formatting | bytes 4194304
  45.0 0.0 copy-done.6
  45.0 0.0 copy-start.1
  45.0 0.0 copy-start
  45.0 0.7 %copy.33 = f32[64,512]{1,0:T(8,128)} copy(f32[64,512]{1,0:T(8,128)S(1)} %copy-done.6) | data formatting | bytes 262144
  45.6 0.0 copy-done.5
  45.6 0.7 %copy.34 = f32[64,512]{1,0:T(8,128)} copy(f32[64,512]{1,0:T(8,128)S(1)} %copy-done.5) | data formatting | bytes 262144
  46.3 0.0 copy-done.4
  46.3 0.7 %copy.35 = f32[256,256]{1,0:T(8,128)} copy(f32[256,256]{1,0:T(8,128)S(1)} %copy-done.4) | data formatting | bytes 524288
  47.0 0.0 copy-done.3
  47.0 0.7 %copy.36 = f32[256,256]{1,0:T(8,128)} copy(f32[256,256]{1,0:T(8,128)S(1)} %copy-done.3) | data formatting | bytes 524288
  47.7 0.0 copy-done.2
  47.7 0.7 %copy.37 = f32[256,256]{1,0:T(8,128)} copy(f32[256,256]{1,0:T(8,128)S(1)} %copy-done.2) | data formatting | bytes 524288
  48.4 0.0 copy-done.1
  48.4 0.8 %copy.38 = f32[1024,128]{1,0:T(8,128)} copy(f32[1024,128]{1,0:T(8,128)S(1)} %copy-done.1) | data formatting | bytes 1048576
  49.2 0.0 copy-done
  49.2 0.8 %copy.39 = f32[1024,128]{1,0:T(8,128)} copy(f32[1024,128]{1,0:T(8,128)S(1)} %copy-done) | data formatting | bytes 1048576
Async XLA Ops:
  41.8 3.2 %copy-start.6 = (f32[64,512]{1,0:T(8,128)S(1)}, f32[64,512]{1,0:T(8,128)}, u32[]{:S(2)}) copy-start(f32[64,512]{1,0:T(8,128)} %get-tuple-element.17) | copy-start | bytes 393220
  41.8 3.9 %copy-start.5 = (f32[64,512]{1,0:T(8,128)S(1)}, f32[64,512]{1,0:T(8,128)}, u32[]{:S(2)}) copy-start(f32[64,512]{1,0:T(8,128)} %get-tuple-element.18) | copy-start | bytes 393220
  41.8 4.5 %copy-start.4 = (f32[256,256]{1,0:T(8,128)S(1)}, f32[256,256]{1,0:T(8,128)}, u32[]{:S(2)}) copy-start(f32[256,256]{1,0:T(8,128)} %get-tuple-element.19) | copy-start | bytes 786436
  41.8 5.2 %copy-start.3 = (f32[256,256]{1,0:T(8,128)S(1)}, f32[256,256]{1,0:T(8,128)}, u32[]{:S(2)}) copy-start(f32[256,256]{1,0:T(8,128)} %get-tuple-element.20) | copy-start | bytes 786436
  41.8 5.9 %copy-start.2 = (f32[256,256]{1,0:T(8,128)S(1)}, f32[256,256]{1,0:T(8,128)}, u32[]{:S(2)}) copy-start(f32[256,256]{1,0:T(8,128)} %get-tuple-element.21) | copy-start | bytes 786436
  45.0 3.4 %copy-start.1 = (f32[1024,128]{1,0:T(8,128)S(1)}, f32[1024,128]{1,0:T(8,128)}, u32[]{:S(2)}) copy-start(f32[1024,128]{1,0:T(8,128)} %get-tuple-element.22) | copy-start | bytes 1572868
  45.0 4.2 %copy-start = (f32[1024,128]{1,0:T(8,128)S(1)}, f32[1024,128]{1,0:T(8,128)}, u32[]{:S(2)}) copy-start(f32[1024,128]{1,0:T(8,128)} %get-tuple-element.23) | copy-start | bytes 1572868

commit v2 on v1

--- a/solution.py
+++ b/solution.py
@@ -408,7 +408,7 @@
     return (single(left[1], right[0]) + single(left[0], right[1])) + single(left[0], right[0])
 
 
-def fused_kernel(chunks, *refs):
+def fused_kernel(plan, *refs):
     (
         two_hbm,
         one_hbm,
@@ -428,15 +428,16 @@
         grad_panel_one_hbm,
     ) = refs[:16]
     (
-        out_below,
-        out_left_two,
-        out_left_one,
-        out_diag_two,
-        out_diag_one,
-        out_cross,
-        out_panel_two,
-        out_panel_one,
-    ) = refs[16:24]
+        acc,
+        panel_out,
+        half_two,
+        next_cross,
+        middle_one,
+        inverse_one,
+        grad_left,
+        left_high,
+        left_low,
+    ) = refs[16:25]
     (
         two,
         one,
@@ -447,18 +448,13 @@
         grad_two,
         grad_one,
         grad_cross,
-        grad_left,
-        acc,
         full_two,
         full_one,
-        solved,
         solved_high,
         solved_low,
-        left_high,
-        left_low,
         below_high,
         below_low,
-        inverses,
+        inverse_two,
         crossed,
         pre,
         partial,
@@ -471,13 +467,9 @@
         lefts_core,
         lefts_send,
         lefts_x,
-        sym,
-        next_cross,
+        sym_two,
         cross_t,
-        halves,
-        panel_out,
         load_sem,
-        store_sem,
         y_send,
         y_recv,
         z_send,
@@ -486,12 +478,10 @@
         w_recv,
         l_send,
         l_recv,
-    ) = refs[24:]
+    ) = refs[25:]
     size = two.shape[0]
     rows, width = grad_panel_two_hbm.shape
     share = grad_left.shape[1]
-    half = rows // 2
-    step = half // chunks
     quarter = width // 2
     at_row, at_col, at_depth = (lax.axis_index(name) for name in ("row", "col", "depth"))
     core = lax.rem(at_row, 2)
@@ -515,9 +505,8 @@
     pan_two = load(panel_two_hbm, panels.at[:, :width])
     pan_one = load(panel_one_hbm, panels.at[:, width:])
     own_one = load(grad_panel_one_hbm, full_one.at[:, :width])
+    block_loads = [load(two_hbm, two), load(one_hbm, one)]
     small_loads = [
-        load(two_hbm, two),
-        load(one_hbm, one),
         load(cross_hbm, cross),
         load(grad_two_hbm, grad_two),
         load(grad_one_hbm, grad_one),
@@ -553,27 +542,33 @@
 
     fulls = (full_two, full_one)
     y_copies = []
+    places = []
     for panel, source in enumerate((grad_panel_two_hbm, grad_panel_one_hbm)):
-        for at in range(chunks):
-            place = pl.ds(pl.multiple_of(part * half + at * step, step), step)
+        forwarded, direct = plan[panel]
+        extent = sum(forwarded)
+        begin = 0
+        for at, count in enumerate(forwarded + direct):
+            if at == len(forwarded):
+                begin = 2 * extent
+            start = part * extent + begin if at < len(forwarded) else begin
+            place = pl.ds(pl.multiple_of(start, 8), count)
+            begin += count
+            at = len(y_copies)
             y_copies.append(
-                send(
-                    source.at[place, :],
-                    fulls[panel].at[place, width:],
-                    (y_send, y_recv),
-                    panel * chunks + at,
-                    to_y,
-                )
+                send(source.at[place, :], fulls[panel].at[place, width:], (y_send, y_recv), at, to_y)
             )
+            places.append((panel, place))
+    order = list(range(len(plan[0][0]))) + [
+        len(plan[0][0]) + len(plan[0][1]) + at for at in range(len(plan[1][0]))
+    ]
     z_copies = []
 
     def forward():
-        at = len(z_copies)
+        at = order[len(z_copies)]
         y_copies[at].wait_recv()
-        panel, chunk = divmod(at, chunks)
-        place = pl.ds(pl.multiple_of(part * half + chunk * step, step), step)
+        panel, place = places[at]
         piece = fulls[panel].at[place, width:]
-        z_copies.append(send(piece, piece, (z_send, z_recv), at, to_z))
+        z_copies.append(send(piece, piece, (z_send, z_recv), len(z_copies), to_z))
 
     mine = pl.ds(pl.multiple_of(core * quarter, quarter), quarter)
     theirs = pl.ds(pl.multiple_of((1 - core) * quarter, quarter), quarter)
@@ -644,84 +639,86 @@
     )
     w_core(0)
 
-    for copy in small_loads:
+    for copy in block_loads:
         copy.wait()
     grid_rows, grid_cols = grid_of(size)
     scale = jnp.where(
         grid_rows > grid_cols, 1.0, jnp.where(grid_rows == grid_cols, 0.5, 0.0)
     )
-    events = {1: forward, 2: lambda: w_x(0), 3: forward, 5: forward, 6: lambda: w_y(0)}
+    events = {
+        1: lambda: w_x(0),
+        2: forward,
+        4: forward,
+        6: lambda: (forward(), w_y(0)),
+    }
     mid = size // 2
     blocks = []
     for ref in (two, one):
         blocks += [ref[:mid, :mid], ref[mid:, mid:]]
     found = invert_steps(blocks, events)
-    for at, ref in enumerate((two, one)):
+    for at, (ref, inverse) in enumerate(((two, inverse_two), (one, inverse_one))):
         step_product = small(ref[mid:, :mid], found[2 * at])
-        inverses[at, :mid, :mid] = found[2 * at]
-        inverses[at, mid:, mid:] = found[2 * at + 1]
-        inverses[at, :mid, mid:] = jnp.zeros((mid, size - mid), jnp.float32)
-        inverses[at, mid:, :mid] = -small(found[2 * at + 1], step_product)
-    while len(z_copies) < chunks:
-        forward()
+        inverse[:mid, :mid] = found[2 * at]
+        inverse[mid:, mid:] = found[2 * at + 1]
+        inverse[:mid, mid:] = jnp.zeros((mid, size - mid), jnp.float32)
+        inverse[mid:, :mid] = -small(found[2 * at + 1], step_product)
+    forward()
 
     def local_rows(values):
         near = jnp.where(first, values[:width, :], values[width:, :])
         away = jnp.where(first, values[width:, :], values[:width, :])
         return jnp.concatenate([near, away], axis=0)
 
-    inverse_two = inverses[0]
-    right_two = split(local_rows(inverse_two))
-
-    def solve_two(begin):
-        place = pl.ds(pl.multiple_of(begin, half), half)
+    def own_columns(values):
+        return jnp.where(first, values[:, :width], values[:, width:])
+
+    right_two = split(local_rows(inverse_two[...]))
+
+    def solve_two(begin, count):
+        place = pl.ds(pl.multiple_of(begin, 8), count)
         pieces = split(full_two[place, :])
         off = thrice(
             tuple(piece[:, width:] for piece in pieces), split(panels[place, :]), (0, 0)
         )
         total = thrice(pieces, right_two)
-        solved[place, :size] = total
+        panel_out[0, place, :] = own_columns(total)
         high, low = split(total)
         solved_high[place, :size] = high
         solved_low[place, :size] = low
         return off
 
-    off_near = solve_two(part * half)
+    half = rows // 2
+    off_near = solve_two(part * half, half)
+    for copy in small_loads:
+        copy.wait()
+    split_cross = split(cross[...])
+    split_two = split(inverse_two[...])
+    split_one = split(inverse_one[...])
+    crossed_one = thrice(split_cross, split_one)
+    crossed[...] = thrice(split_two, split_cross)
     forward()
-    crossed[0] = small(cross[...], inverses[1])
-    crossed[1] = small(inverse_two, cross[...])
-    pre[0] = small(two[...], grad_two[...], (0, 0))
-    pre[1] = small(one[...], grad_one[...], (0, 0))
-    for at in range(chunks):
+    pre[0] = thrice(split(two[...]), split(grad_two[...]), (0, 0))
+    pre[1] = thrice(split(one[...]), split(grad_one[...]), (0, 0))
+    right_one = split(jnp.concatenate([local_rows(inverse_one[...]), -crossed_one], axis=0))
+    below_load.wait()
+    high, low = split(below[...])
+    below_high[...] = high
+    below_low[...] = low
+    forward()
+    for at in range(len(plan[0][0])):
         z_copies[at].wait_recv()
-    off_far = solve_two((1 - part) * half)
+    off_far = solve_two((1 - part) * half, half)
     off = off_near + off_far
     partial[3] = off[:, :width]
     partial[4] = off[:, width:]
     w_core(1)
     forward()
-
-    stores = []
-
-    def store(source, target):
-        copy = pltpu.make_async_copy(source, target, store_sem.at[len(stores)])
-        copy.start()
-        stores.append(copy)
-
-    def own_columns(values):
-        return jnp.where(first, values[:, :width], values[:, width:])
-
-    panel_out[0] = own_columns(solved[:, :size])
-    store(panel_out.at[0], out_panel_two)
-    below_load.wait()
-    high, low = split(below[...])
-    below_high[...] = high
-    below_low[...] = low
     for copy in left_loads:
         copy.wait()
     high, low = split(left[...])
     left_high[...] = high
     left_low[...] = low
+    forward()
     w_x(1)
     l_waits = {}
 
@@ -754,106 +751,153 @@
         l_waits["x", panel].wait_recv()
         return (lefts[panel, side, core] + lefts_core[panel, side]) + lefts_x[panel]
 
-    tile = rows // 4
-
-    def below_of(panel):
+    tiles = 4
+    tile = rows // tiles
+
+    def below_of(panel, at):
         columns = pl.ds(panel * size, size)
-        rights = (left_high[columns, :], left_low[columns, :])
-        for at in range(4):
-            place = pl.ds(at * tile, tile)
-            acc[place, :] = acc[place, :] - thrice(
-                (solved_high[place, columns], solved_low[place, columns]), rights
-            )
-
-    lefts_of(0)
-    forward()
-    acc_load.wait()
-    below_of(0)
-    lefts_away(0)
-    forward()
-    w_y(1)
-
-    right_one = split(
-        jnp.concatenate([local_rows(inverses[1]), -crossed[0]], axis=0)
-    )
-
-    def solve_one(begin):
-        place = pl.ds(pl.multiple_of(begin, half), half)
+        place = pl.ds(at * tile, tile)
+        acc[place, :] = acc[place, :] - thrice(
+            (solved_high[place, columns], solved_low[place, columns]),
+            (left_high[columns, :], left_low[columns, :]),
+        )
+
+    def solve_one(begin, count):
+        place = pl.ds(pl.multiple_of(begin, 8), count)
         pieces = split(full_one[place, :])
         off = thrice(
             tuple(piece[:, width:] for piece in pieces), split(panels[place, width:]), (0, 0)
         )
-        lefts_of_it = tuple(
+        both = tuple(
             jnp.concatenate([piece, before[place, :size]], axis=1)
             for piece, before in zip(pieces, (solved_high, solved_low))
         )
-        total = thrice(lefts_of_it, right_one)
-        solved[place, size:] = total
+        total = thrice(both, right_one)
+        panel_out[1, place, :] = own_columns(total)
         high, low = split(total)
         solved_high[place, size:] = high
         solved_low[place, size:] = low
         return off
 
-    off_near = solve_one(part * half)
+    lefts_of(0)
+    extent = sum(plan[1][0])
+    off_near = solve_one(part * extent, extent)
+    w_y(1)
+    lefts_away(0)
+    for at in range(len(plan[0][0]), len(order)):
+        z_copies[at].wait_recv()
+    off_far = solve_one((1 - part) * extent, extent)
+    off = off_near + off_far
+    if plan[1][1]:
+        for at in range(len(plan[1][1])):
+            y_copies[len(y_copies) - 1 - at].wait_recv()
+        off = off + solve_one(2 * extent, sum(plan[1][1]))
+    partial[5] = off
+    w_core(2)
+    lefts_of(1)
+    w_x(2)
     w_last(0)
-    for at in range(chunks, 2 * chunks):
-        z_copies[at].wait_recv()
-    off_far = solve_one((1 - part) * half)
-    partial[5] = off_near + off_far
-    w_core(2)
-    panel_out[1] = own_columns(solved[:, size:])
-    store(panel_out.at[1], out_panel_one)
+    acc_load.wait()
+    below_of(0, 0)
+    lefts_away(1)
+    below_of(0, 1)
+    below_of(0, 2)
+    w_y(2)
     w_last(1)
-    w_x(2)
-    lefts_of(1)
-    w_y(2)
+    below_of(0, 3)
     w_done(0)
     w_done(1)
 
     inner = scale * (pre[0] - joined_at(0, 3))
-    middle = inner + inner.T
-    cross_gram = small(inverse_two, joined_at(1, 4), (0, 0))
-    spread = small(
-        inverse_two,
-        small(middle, jnp.concatenate([inverse_two, crossed[1]], axis=1)),
+    middle = split(inner + inner.T)
+    cross_gram = thrice(split_two, split(joined_at(1, 4)), (0, 0))
+    spread = thrice(
+        split_two,
+        split(
+            thrice(
+                middle, split(jnp.concatenate([inverse_two[...], crossed[...]], axis=1))
+            )
+        ),
         (0, 0),
     )
-    sym[0] = spread[:, :size]
-    halves[0] = scale * sym[0]
-    store(halves.at[0], out_diag_two)
-    following = grad_cross[...] - cross_gram - spread[:, size:]
-    next_cross[...] = small(following, inverses[1])
-    store(next_cross, out_cross)
-    cross_t[...] = next_cross[...].T
-    lefts_away(1)
+    sym_two[...] = spread[:, :size]
+    half_two[...] = scale * spread[:, :size]
+    following = split(grad_cross[...] - cross_gram - spread[:, size:])
+    found = thrice(following, split_one)
+    next_cross[...] = found
+    cross_t[...] = found.T
     ready = pre[1] - (
-        small(following, cross[...], (0, 0)) - small(cross[...], cross_gram, (0, 0))
-    )
+        thrice(following, split_cross, (0, 0)) - thrice(split_cross, split(cross_gram), (0, 0))
+    )
+    for at in range(tiles):
+        below_of(1, at)
     w_last(2)
-    below_of(1)
-    store(acc, out_below)
     mine_rows = pl.ds(pl.multiple_of(at_row * share, share), share)
     for copy in grad_left_loads:
         copy.wait()
-    head = split(jnp.concatenate([sym[0, mine_rows, :], next_cross[mine_rows, :]], axis=1))
+    head = split(jnp.concatenate([sym_two[mine_rows, :], next_cross[mine_rows, :]], axis=1))
     grad_left[0] = (grad_left[0] - lefts_end(0)) - thrice(
         head, (left_high[...], left_low[...])
     )
-    store(grad_left.at[0], out_left_two)
     grad_left[1] = (grad_left[1] - lefts_end(1)) - thrice(
         split(cross_t[mine_rows, :]), (left_high[:size], left_low[:size])
     )
     w_done(2)
     inner = scale * (ready - joined_at(2, 5))
-    sym[1] = small(inverses[1], small(inner + inner.T, inverses[1]), (0, 0))
-    grad_left[1] = grad_left[1] - thrice(
-        split(sym[1, mine_rows, :]), (left_high[size:], left_low[size:])
-    )
-    store(grad_left.at[1], out_left_one)
-    halves[1] = scale * sym[1]
-    store(halves.at[1], out_diag_one)
+    middle_one[...] = inner + inner.T
     for copy in sends:
         copy.wait_send()
+
+
+def tail_kernel(*refs):
+    (
+        acc,
+        panel_out,
+        half_two,
+        next_cross,
+        middle_one,
+        inverse_one,
+        grad_left,
+        left_high,
+        left_low,
+    ) = refs[:9]
+    (
+        out_below,
+        out_left_two,
+        out_left_one,
+        out_diag_two,
+        out_diag_one,
+        out_cross,
+        out_panel_two,
+        out_panel_one,
+    ) = refs[9:17]
+    sym_one, half_one, last, store_sem = refs[17:]
+    size = sym_one.shape[0]
+    share = last.shape[0]
+    stores = []
+
+    def store(source, target):
+        copy = pltpu.make_async_copy(source, target, store_sem.at[len(stores)])
+        copy.start()
+        stores.append(copy)
+
+    store(acc, out_below)
+    store(panel_out.at[0], out_panel_two)
+    store(panel_out.at[1], out_panel_one)
+    store(half_two, out_diag_two)
+    store(next_cross, out_cross)
+    store(grad_left.at[0], out_left_two)
+    inverse = split(inverse_one[...])
+    found = thrice(inverse, split(thrice(split(middle_one[...]), inverse)), (0, 0))
+    sym_one[...] = found
+    rows, cols = grid_of(size)
+    half_one[...] = jnp.where(rows > cols, found, jnp.where(rows == cols, 0.5 * found, 0.0))
+    store(half_one, out_diag_one)
+    mine_rows = pl.ds(pl.multiple_of(lax.axis_index("row") * share, share), share)
+    last[...] = grad_left[1] - thrice(
+        split(sym_one[mine_rows, :]), (left_high[size:, :], left_low[size:, :])
+    )
+    store(last, out_left_one)
     for copy in stores:
         copy.wait()
 
@@ -892,8 +936,14 @@
     rows, width = arrays[14].shape
     columns = below.shape[1]
     share = grad_left.shape[0]
-    chunks = 4
     quarter = width // 2
+    piece = rows // 8
+    plan = (
+        ([piece] * 4, []),
+        ([piece] * 2 + [piece // 2] * 2, [piece] * 2),
+    )
+    y_count = sum(len(go) + len(stay) for go, stay in plan)
+    z_count = sum(len(go) for go, _ in plan)
 
     def real(*shape):
         return pltpu.VMEM(shape, jnp.float32)
@@ -914,19 +964,14 @@
         real(size, size),
         real(size, size),
         real(size, size),
-        real(2, share, columns),
-        real(rows, columns),
         real(rows, size),
         real(rows, size),
-        real(rows, 2 * size),
         short(rows, 2 * size),
         short(rows, 2 * size),
-        short(2 * size, columns),
-        short(2 * size, columns),
         short(rows, columns),
         short(rows, columns),
-        real(2, size, size),
-        real(2, size, size),
+        real(size, size),
+        real(size, size),
         real(2, size, size),
         real(6, width, width),
         real(6, quarter, width),
@@ -938,25 +983,46 @@
         real(2, 2, share, columns),
         real(2, share, columns),
         real(2, share, columns),
-        real(2, size, size),
         real(size, size),
         real(size, size),
-        real(2, size, size),
-        real(2, rows, width),
         pltpu.SemaphoreType.DMA((16,)),
-        pltpu.SemaphoreType.DMA((8,)),
-        pltpu.SemaphoreType.DMA((2 * chunks,)),
-        pltpu.SemaphoreType.DMA((2 * chunks,)),
-        pltpu.SemaphoreType.DMA((2 * chunks,)),
-        pltpu.SemaphoreType.DMA((2 * chunks,)),
+        pltpu.SemaphoreType.DMA((y_count,)),
+        pltpu.SemaphoreType.DMA((y_count,)),
+        pltpu.SemaphoreType.DMA((z_count,)),
+        pltpu.SemaphoreType.DMA((z_count,)),
         pltpu.SemaphoreType.DMA((15,)),
         pltpu.SemaphoreType.DMA((15,)),
         pltpu.SemaphoreType.DMA((6,)),
         pltpu.SemaphoreType.DMA((6,)),
     ]
     anywhere = pl.BlockSpec(memory_space=pl.ANY)
+    near = pl.BlockSpec(memory_space=pltpu.VMEM)
+    far = pl.BlockSpec(memory_space=pltpu.HBM)
+    kept = pl.pallas_call(
+        lambda *refs: fused_kernel(plan, *refs),
+        out_shape=[
+            real(rows, columns),
+            real(2, rows, width),
+            real(size, size),
+            real(size, size),
+            real(size, size),
+            real(size, size),
+            real(2, share, columns),
+            short(2 * size, columns),
+            short(2 * size, columns),
+        ],
+        in_specs=[far] * 16,
+        out_specs=[near] * 9,
+        scratch_shapes=scratch,
+        compiler_params=pltpu.CompilerParams(
+            collective_id=0, has_side_effects=True, vmem_limit_bytes=40 << 20
+        ),
+        cost_estimate=pl.CostEstimate(
+            flops=24 * rows * size * columns, bytes_accessed=16 * rows * columns, transcendentals=0
+        ),
+    )(*[pltpu.with_memory_space_constraint(values, pltpu.HBM) for values in arrays])
     return pl.pallas_call(
-        lambda *refs: fused_kernel(chunks, *refs),
+        tail_kernel,
         out_shape=[
             outs(rows, columns),
             outs(share, columns),
@@ -967,14 +1033,19 @@
             outs(rows, width),
             outs(rows, width),
         ],
-        in_specs=[anywhere] * 16,
+        in_specs=[near] * 9,
         out_specs=[anywhere] * 8,
-        scratch_shapes=scratch,
-        compiler_params=pltpu.CompilerParams(collective_id=0, has_side_effects=True),
+        scratch_shapes=[
+            real(size, size),
+            real(size, size),
+            real(share, columns),
+            pltpu.SemaphoreType.DMA((8,)),
+        ],
+        compiler_params=pltpu.CompilerParams(vmem_limit_bytes=8 << 20),
         cost_estimate=pl.CostEstimate(
-            flops=24 * rows * size * columns, bytes_accessed=16 * rows * columns, transcendentals=0
+            flops=12 * size**3, bytes_accessed=8 * rows * columns, transcendentals=0
         ),
-    )(*arrays)
+    )(*[pltpu.with_memory_space_constraint(values, pltpu.VMEM) for values in kept])
 
 
 def fits(mesh):

time: 50.2 us -> 36.7 us (0.73)
  local copies, waits for them, and re-layouts: 8.2 us -> 0 us
  Pallas kernels: 41.1 us -> 35.7 us
    unnamed x22 -> x0, local copies, waits for them, and re-layouts: 8.2 us -> none
    pallas_call x1 -> x2, Pallas kernels: 41.1 us -> 35.7 us  [the longest x1 33.7 us: fused(): pl.pallas_call(lambda *refs: fused_kernel(plan, *refs), out_shape=[real(r...]
where the time goes in v2:
time: 36.7 us; the launch traced here: 36.5 us
  Pallas kernels  35.7 us (97%)
  between operations  0.81 us (2%)
    pallas_call x1, Pallas kernels, fused(): pl.pallas_call(lambda *refs: fused_kernel(plan, *refs), out_shape=[real(r...  33.7 us
    pallas_call x1, Pallas kernels, fused(): pl.pallas_call(tail_kernel, out_shape=[outs(rows, columns), outs(share, c...  2.07 us

profile of v2, /device:TPU:0, one launch (start us, length us, event | category | flops | bytes accessed | tf_op | source)
XLA Modules:
  0.0 36.5 jit_solution(8250259572991950900)
XLA Ops:
  0.6 33.7 %shard_map.215 = (f32[1024,512]{1,0:T(8,128)S(1)}, f32[2,1024,128]{2,1,0:T(8,128)S(1)}, f32[256,256]{1,0:T(8,128)S(1)}, f32[256,256]{1,0:T(8,128)S(1)}, f32[256,...) custom-call(f32[256,256]{1,0:T(8,128)} %refs_0_.1, ...), custom_call_target="tpu_custom_call" | custom-call | flops 3221225472 | bytes 8388608 | tf_op jit(solution)/shard_map/pallas_call | solution.py:1001
  34.3 2.1 %shard_map.216 = (f32[1024,512]{1,0:T(8,128)}, f32[64,512]{1,0:T(8,128)}, f32[64,512]{1,0:T(8,128)}, f32[256,256]{1,0:T(8,128)}, f32[256,256]{1,0:T(8,128)}, /*i...) custom-call(f32[1024,512]{1,0:T(8,128)S(1)} %get-tuple-element.17.refs_0_, ...), custom_call_target="tpu_custom_call" | custom-call | flops 201326592 | bytes 4194304 | tf_op jit(solution)/shard_map/pallas_call | solution.py:1024
